TPU v7x, 32 devices: a whole 2x2x4 slice. The times are simulated.
32 devices in a mesh: row: 4 (over z), col: 8 (over y, x, core).
Axes of the slice: x: 2, y: 2, z: 4, core: 2. Of those that a mesh axis runs over, the one named last changes fastest.
Arguments:
- points: float32 [16, 32768], P(None, ('row', 'col')), may hold values from -6 to 6
- inverse_scales: float32 [16], replicated, may hold values from 0.05 to 31.255105
- probe_signs: int32 [32768, 128], P(('row', 'col')), may hold values 0 or 1
Outputs:
- trace_terms: float32 [128], replicated
- logdet_terms: float32 [128], replicated
All inputs are finite; a program needn't handle non-finite values. No bound on the sum of `probe_signs` on one device may be relied on, other than what follows from the above.
Results may differ from a plain program's by a relative error of at most 0.0014.
Values may be sent and summed in bfloat16 or wider, within the bound.
A program may use at most 128 MiB of HBM per device.

v0:
```python
import math
import jax
import jax.numpy as jnp
from jax import lax
from jax.sharding import PartitionSpec as P

STEPS = 3
epsilon = 1e-06
noise_level = 1.0
jacobi_sweeps = 6


def kernel_block(left_points, right_points):
    cross_term = lax.dot_general(
        left_points,
        right_points,
        (((0,), (0,)), ((), ())),
        precision=lax.Precision.HIGHEST,
        preferred_element_type=jnp.float32,
    )
    left_norms = jnp.sum(left_points * left_points, axis=0)
    right_norms = jnp.sum(right_points * right_points, axis=0)
    distance = jnp.maximum(left_norms[:, None] + right_norms[None, :] - 2.0 * cross_term, 0.0)
    return jnp.exp(-0.5 * distance).astype(jnp.bfloat16)


def form_blocks(row_points, col_points):
    total_rows = row_points.shape[1]
    block_rows = math.gcd(total_rows, 512)
    blocked = row_points.reshape(
        row_points.shape[0], total_rows // block_rows, block_rows
    ).transpose(1, 0, 2)
    stacked = lax.map(lambda block_points: kernel_block(block_points, col_points), blocked)
    return stacked.reshape(total_rows, col_points.shape[1])


def log_weight(alpha_list, beta_list):
    degree = len(alpha_list)
    width_probes = alpha_list[0].shape[0]
    zeros_row = jnp.zeros((width_probes,), jnp.float32)
    ones_row = jnp.ones((width_probes,), jnp.float32)
    matrix = []
    vectors = []
    for first_idx in range(degree):
        entries = []
        basis_row = []
        for second_idx in range(degree):
            if first_idx == second_idx:
                entries.append(alpha_list[first_idx])
                basis_row.append(ones_row)
            elif abs(first_idx - second_idx) == 1:
                entries.append(beta_list[min(first_idx, second_idx)])
                basis_row.append(zeros_row)
            else:
                entries.append(zeros_row)
                basis_row.append(zeros_row)
        matrix.append(entries)
        vectors.append(basis_row)
    for sweep_index in range(jacobi_sweeps):
        for first_idx in range(degree):
            for second_idx in range(first_idx + 1, degree):
                coupling = matrix[first_idx][second_idx]
                rotate_by = 0.5 * jnp.arctan2(
                    2.0 * coupling, matrix[second_idx][second_idx] - matrix[first_idx][first_idx]
                )
                cosine = jnp.cos(rotate_by)
                sine_val = jnp.sin(rotate_by)
                for row_idx in range(degree):
                    left_val = matrix[row_idx][first_idx]
                    right_val = matrix[row_idx][second_idx]
                    matrix[row_idx][first_idx] = cosine * left_val - sine_val * right_val
                    matrix[row_idx][second_idx] = sine_val * left_val + cosine * right_val
                    left_vec = vectors[row_idx][first_idx]
                    right_vec = vectors[row_idx][second_idx]
                    vectors[row_idx][first_idx] = cosine * left_vec - sine_val * right_vec
                    vectors[row_idx][second_idx] = sine_val * left_vec + cosine * right_vec
                for col_idx in range(degree):
                    upper_val = matrix[first_idx][col_idx]
                    lower_val = matrix[second_idx][col_idx]
                    matrix[first_idx][col_idx] = cosine * upper_val - sine_val * lower_val
                    matrix[second_idx][col_idx] = sine_val * upper_val + cosine * lower_val
    total = zeros_row
    for index_k in range(degree):
        total = total + vectors[0][index_k] * vectors[0][index_k] * jnp.log(
            matrix[index_k][index_k]
        )
    return total


def per_device(points, inverse_scales, probe_signs):
    scaled = points * inverse_scales[:, None]
    row_points = lax.all_gather(scaled, "col", axis=1, tiled=True)
    col_points = lax.all_gather(scaled, "row", axis=1, tiled=True)
    cached = form_blocks(row_points, col_points)
    direction = 2.0 * probe_signs.astype(jnp.float32) - 1.0
    basis_prev = jnp.zeros_like(direction)
    alpha_list = []
    beta_list = []
    for lanczos_step in range(STEPS):
        squares = lax.psum(jnp.sum(direction * direction, axis=0), ("row", "col"))
        vector_half = direction.astype(jnp.bfloat16)
        gathered = lax.all_gather(vector_half, "col", axis=0, tiled=True)
        image = (
            lax.psum_scatter(
                lax.dot_general(
                    cached, gathered, (((0,), (0,)), ((), ())), preferred_element_type=jnp.float32
                ).astype(jnp.bfloat16),
                "row",
                scatter_dimension=0,
                tiled=True,
            ).astype(jnp.float32)
            + noise_level * direction
        )
        curvature = lax.psum(jnp.sum(direction * image, axis=0), ("row", "col"))
        beta_now = jnp.sqrt(squares + epsilon)
        alpha_now = curvature / (beta_now * beta_now)
        alpha_list.append(alpha_now)
        beta_list.append(beta_now)
        if lanczos_step + 1 < STEPS:
            basis_now = direction / beta_now
            direction = image / beta_now - alpha_now * basis_now - beta_now * basis_prev
            basis_prev = basis_now
    logdet_terms = log_weight(alpha_list, beta_list[1:])
    return (alpha_list[0], logdet_terms)


def solution(mesh):
    in_specs = (P(None, ("row", "col")), P(), P(("row", "col"), None))
    out_specs = (P(), P())
    return jax.shard_map(
        per_device, mesh=mesh, in_specs=in_specs, out_specs=out_specs, check_vma=False
    )
```

profile of v0, /device:TPU:0, one launch (start us, length us, event | category | flops | bytes accessed | tf_op | source)
XLA Modules:
  0.0 559.0 jit_solution(14007900071963346204)
XLA Ops:
  10.0 15.6 %all_gather.16 = f32[16,4096]{1,0:T(8,128)S(1)} all-gather(f32[16,1024]{1,0:T(8,128)S(1)} %broadcast_multiply_fusion), channel_id=1, replica_groups=mesh['row'=4,'col'=8] {'row'}, dimensions={1}, use_global_device_ids=true | all-gather | bytes 327680 | tf_op jit(solution)/shard_map/all_gather | solution.py:93
  25.7 11.0 %all_gather.15 = f32[16,8192]{1,0:T(8,128)S(1)} all-gather(f32[16,1024]{1,0:T(8,128)S(1)} %broadcast_multiply_fusion), channel_id=1, replica_groups=mesh['row'=4,'col'=8] {'col'}, dimensions={1}, use_global_device_ids=true | all-gather | bytes 589824 | tf_op jit(solution)/shard_map/all_gather | solution.py:92
  36.8 163.7 %while.12 = (s32[]{:T(128)}, bf16[16,512,4096]{2,1,0:T(8,128)(2,1)}, f32[16,16,512]{2,1,0:T(8,128)S(1)}, f32[4096]{0:T(1024)S(1)}, f32[16,4096]{1,0:T(8,128)S(1)}, /*index=5*/s32[]{:T(128)}) while((s32[]{:T(128)}, bf16[16,512,4096]{2,1,0:T(8,128)(2,1)}, f32[16,16,512]{2,1,0:T(8,128)S(1)}, f32[4096]{0:T(1024)S(1)}, f32[16,4096]{1,0:T(8,128)S(1)}, ...), condition=%wide.region_3.4_spmd, body=%wide.region_1.3_spmd.sunk | while | flops 415251968 | bytes 4543561 | solution.py:33
  36.8 10.2 %fusion.25 = bf16[16,512,4096]{2,1,0:T(8,128)(2,1)} fusion(bf16[16,512,4096]{2,1,0:T(8,128)(2,1)} %get-tuple-element.127, s32[]{:T(128)} %get-tuple-element.126, f32[16,4096]{1,0:T(8,128)S(1)} %get-tuple-element.136, f32[4096]{0:T(1024)S(1)} %get-tuple-element.135, f32[512]{0:T(512)S(1)} %fusion.24, f32[16,16,512]{2,1,0:T(8,128)S(1)} %get-tuple-element.134), kind=kOutput, calls=%fused_computation.2.clone.1 | convolution fusion | flops 415236096 | bytes 4508672 | tf_op jit(solution)/shard_map/while/body/eval_jaxpr/dot_general | solution.py:14
  47.1 10.2 %fusion.25 = bf16[16,512,4096]{2,1,0:T(8,128)(2,1)} fusion(bf16[16,512,4096]{2,1,0:T(8,128)(2,1)} %get-tuple-element.127, s32[]{:T(128)} %get-tuple-element.126, f32[16,4096]{1,0:T(8,128)S(1)} %get-tuple-element.136, f32[4096]{0:T(1024)S(1)} %get-tuple-element.135, f32[512]{0:T(512)S(1)} %fusion.24, f32[16,16,512]{2,1,0:T(8,128)S(1)} %get-tuple-element.134), kind=kOutput, calls=%fused_computation.2.clone.1 | convolution fusion | flops 415236096 | bytes 4508672 | tf_op jit(solution)/shard_map/while/body/eval_jaxpr/dot_general | solution.py:14
  57.3 10.2 %fusion.25 = bf16[16,512,4096]{2,1,0:T(8,128)(2,1)} fusion(bf16[16,512,4096]{2,1,0:T(8,128)(2,1)} %get-tuple-element.127, s32[]{:T(128)} %get-tuple-element.126, f32[16,4096]{1,0:T(8,128)S(1)} %get-tuple-element.136, f32[4096]{0:T(1024)S(1)} %get-tuple-element.135, f32[512]{0:T(512)S(1)} %fusion.24, f32[16,16,512]{2,1,0:T(8,128)S(1)} %get-tuple-element.134), kind=kOutput, calls=%fused_computation.2.clone.1 | convolution fusion | flops 415236096 | bytes 4508672 | tf_op jit(solution)/shard_map/while/body/eval_jaxpr/dot_general | solution.py:14
  67.5 10.2 %fusion.25 = bf16[16,512,4096]{2,1,0:T(8,128)(2,1)} fusion(bf16[16,512,4096]{2,1,0:T(8,128)(2,1)} %get-tuple-element.127, s32[]{:T(128)} %get-tuple-element.126, f32[16,4096]{1,0:T(8,128)S(1)} %get-tuple-element.136, f32[4096]{0:T(1024)S(1)} %get-tuple-element.135, f32[512]{0:T(512)S(1)} %fusion.24, f32[16,16,512]{2,1,0:T(8,128)S(1)} %get-tuple-element.134), kind=kOutput, calls=%fused_computation.2.clone.1 | convolution fusion | flops 415236096 | bytes 4508672 | tf_op jit(solution)/shard_map/while/body/eval_jaxpr/dot_general | solution.py:14
  77.8 10.2 %fusion.25 = bf16[16,512,4096]{2,1,0:T(8,128)(2,1)} fusion(bf16[16,512,4096]{2,1,0:T(8,128)(2,1)} %get-tuple-element.127, s32[]{:T(128)} %get-tuple-element.126, f32[16,4096]{1,0:T(8,128)S(1)} %get-tuple-element.136, f32[4096]{0:T(1024)S(1)} %get-tuple-element.135, f32[512]{0:T(512)S(1)} %fusion.24, f32[16,16,512]{2,1,0:T(8,128)S(1)} %get-tuple-element.134), kind=kOutput, calls=%fused_computation.2.clone.1 | convolution fusion | flops 415236096 | bytes 4508672 | tf_op jit(solution)/shard_map/while/body/eval_jaxpr/dot_general | solution.py:14
  88.0 10.2 %fusion.25 = bf16[16,512,4096]{2,1,0:T(8,128)(2,1)} fusion(bf16[16,512,4096]{2,1,0:T(8,128)(2,1)} %get-tuple-element.127, s32[]{:T(128)} %get-tuple-element.126, f32[16,4096]{1,0:T(8,128)S(1)} %get-tuple-element.136, f32[4096]{0:T(1024)S(1)} %get-tuple-element.135, f32[512]{0:T(512)S(1)} %fusion.24, f32[16,16,512]{2,1,0:T(8,128)S(1)} %get-tuple-element.134), kind=kOutput, calls=%fused_computation.2.clone.1 | convolution fusion | flops 415236096 | bytes 4508672 | tf_op jit(solution)/shard_map/while/body/eval_jaxpr/dot_general | solution.py:14
  98.2 10.2 %fusion.25 = bf16[16,512,4096]{2,1,0:T(8,128)(2,1)} fusion(bf16[16,512,4096]{2,1,0:T(8,128)(2,1)} %get-tuple-element.127, s32[]{:T(128)} %get-tuple-element.126, f32[16,4096]{1,0:T(8,128)S(1)} %get-tuple-element.136, f32[4096]{0:T(1024)S(1)} %get-tuple-element.135, f32[512]{0:T(512)S(1)} %fusion.24, f32[16,16,512]{2,1,0:T(8,128)S(1)} %get-tuple-element.134), kind=kOutput, calls=%fused_computation.2.clone.1 | convolution fusion | flops 415236096 | bytes 4508672 | tf_op jit(solution)/shard_map/while/body/eval_jaxpr/dot_general | solution.py:14
  108.4 10.2 %fusion.25 = bf16[16,512,4096]{2,1,0:T(8,128)(2,1)} fusion(bf16[16,512,4096]{2,1,0:T(8,128)(2,1)} %get-tuple-element.127, s32[]{:T(128)} %get-tuple-element.126, f32[16,4096]{1,0:T(8,128)S(1)} %get-tuple-element.136, f32[4096]{0:T(1024)S(1)} %get-tuple-element.135, f32[512]{0:T(512)S(1)} %fusion.24, f32[16,16,512]{2,1,0:T(8,128)S(1)} %get-tuple-element.134), kind=kOutput, calls=%fused_computation.2.clone.1 | convolution fusion | flops 415236096 | bytes 4508672 | tf_op jit(solution)/shard_map/while/body/eval_jaxpr/dot_general | solution.py:14
  118.6 10.3 %fusion.25 = bf16[16,512,4096]{2,1,0:T(8,128)(2,1)} fusion(bf16[16,512,4096]{2,1,0:T(8,128)(2,1)} %get-tuple-element.127, s32[]{:T(128)} %get-tuple-element.126, f32[16,4096]{1,0:T(8,128)S(1)} %get-tuple-element.136, f32[4096]{0:T(1024)S(1)} %get-tuple-element.135, f32[512]{0:T(512)S(1)} %fusion.24, f32[16,16,512]{2,1,0:T(8,128)S(1)} %get-tuple-element.134), kind=kOutput, calls=%fused_computation.2.clone.1 | convolution fusion | flops 415236096 | bytes 4508672 | tf_op jit(solution)/shard_map/while/body/eval_jaxpr/dot_general | solution.py:14
  128.9 10.2 %fusion.25 = bf16[16,512,4096]{2,1,0:T(8,128)(2,1)} fusion(bf16[16,512,4096]{2,1,0:T(8,128)(2,1)} %get-tuple-element.127, s32[]{:T(128)} %get-tuple-element.126, f32[16,4096]{1,0:T(8,128)S(1)} %get-tuple-element.136, f32[4096]{0:T(1024)S(1)} %get-tuple-element.135, f32[512]{0:T(512)S(1)} %fusion.24, f32[16,16,512]{2,1,0:T(8,128)S(1)} %get-tuple-element.134), kind=kOutput, calls=%fused_computation.2.clone.1 | convolution fusion | flops 415236096 | bytes 4508672 | tf_op jit(solution)/shard_map/while/body/eval_jaxpr/dot_general | solution.py:14
  139.2 10.2 %fusion.25 = bf16[16,512,4096]{2,1,0:T(8,128)(2,1)} fusion(bf16[16,512,4096]{2,1,0:T(8,128)(2,1)} %get-tuple-element.127, s32[]{:T(128)} %get-tuple-element.126, f32[16,4096]{1,0:T(8,128)S(1)} %get-tuple-element.136, f32[4096]{0:T(1024)S(1)} %get-tuple-element.135, f32[512]{0:T(512)S(1)} %fusion.24, f32[16,16,512]{2,1,0:T(8,128)S(1)} %get-tuple-element.134), kind=kOutput, calls=%fused_computation.2.clone.1 | convolution fusion | flops 415236096 | bytes 4508672 | tf_op jit(solution)/shard_map/while/body/eval_jaxpr/dot_general | solution.py:14
  149.4 10.2 %fusion.25 = bf16[16,512,4096]{2,1,0:T(8,128)(2,1)} fusion(bf16[16,512,4096]{2,1,0:T(8,128)(2,1)} %get-tuple-element.127, s32[]{:T(128)} %get-tuple-element.126, f32[16,4096]{1,0:T(8,128)S(1)} %get-tuple-element.136, f32[4096]{0:T(1024)S(1)} %get-tuple-element.135, f32[512]{0:T(512)S(1)} %fusion.24, f32[16,16,512]{2,1,0:T(8,128)S(1)} %get-tuple-element.134), kind=kOutput, calls=%fused_computation.2.clone.1 | convolution fusion | flops 415236096 | bytes 4508672 | tf_op jit(solution)/shard_map/while/body/eval_jaxpr/dot_general | solution.py:14
  159.6 10.3 %fusion.25 = bf16[16,512,4096]{2,1,0:T(8,128)(2,1)} fusion(bf16[16,512,4096]{2,1,0:T(8,128)(2,1)} %get-tuple-element.127, s32[]{:T(128)} %get-tuple-element.126, f32[16,4096]{1,0:T(8,128)S(1)} %get-tuple-element.136, f32[4096]{0:T(1024)S(1)} %get-tuple-element.135, f32[512]{0:T(512)S(1)} %fusion.24, f32[16,16,512]{2,1,0:T(8,128)S(1)} %get-tuple-element.134), kind=kOutput, calls=%fused_computation.2.clone.1 | convolution fusion | flops 415236096 | bytes 4508672 | tf_op jit(solution)/shard_map/while/body/eval_jaxpr/dot_general | solution.py:14
  169.9 10.2 %fusion.25 = bf16[16,512,4096]{2,1,0:T(8,128)(2,1)} fusion(bf16[16,512,4096]{2,1,0:T(8,128)(2,1)} %get-tuple-element.127, s32[]{:T(128)} %get-tuple-element.126, f32[16,4096]{1,0:T(8,128)S(1)} %get-tuple-element.136, f32[4096]{0:T(1024)S(1)} %get-tuple-element.135, f32[512]{0:T(512)S(1)} %fusion.24, f32[16,16,512]{2,1,0:T(8,128)S(1)} %get-tuple-element.134), kind=kOutput, calls=%fused_computation.2.clone.1 | convolution fusion | flops 415236096 | bytes 4508672 | tf_op jit(solution)/shard_map/while/body/eval_jaxpr/dot_general | solution.py:14
  180.1 10.2 %fusion.25 = bf16[16,512,4096]{2,1,0:T(8,128)(2,1)} fusion(bf16[16,512,4096]{2,1,0:T(8,128)(2,1)} %get-tuple-element.127, s32[]{:T(128)} %get-tuple-element.126, f32[16,4096]{1,0:T(8,128)S(1)} %get-tuple-element.136, f32[4096]{0:T(1024)S(1)} %get-tuple-element.135, f32[512]{0:T(512)S(1)} %fusion.24, f32[16,16,512]{2,1,0:T(8,128)S(1)} %get-tuple-element.134), kind=kOutput, calls=%fused_computation.2.clone.1 | convolution fusion | flops 415236096 | bytes 4508672 | tf_op jit(solution)/shard_map/while/body/eval_jaxpr/dot_general | solution.py:14
  190.3 10.2 %fusion.25 = bf16[16,512,4096]{2,1,0:T(8,128)(2,1)} fusion(bf16[16,512,4096]{2,1,0:T(8,128)(2,1)} %get-tuple-element.127, s32[]{:T(128)} %get-tuple-element.126, f32[16,4096]{1,0:T(8,128)S(1)} %get-tuple-element.136, f32[4096]{0:T(1024)S(1)} %get-tuple-element.135, f32[512]{0:T(512)S(1)} %fusion.24, f32[16,16,512]{2,1,0:T(8,128)S(1)} %get-tuple-element.134), kind=kOutput, calls=%fused_computation.2.clone.1 | convolution fusion | flops 415236096 | bytes 4508672 | tf_op jit(solution)/shard_map/while/body/eval_jaxpr/dot_general | solution.py:14
  200.5 29.2 %convolution_convert_fusion.2 = bf16[4096,128]{1,0:T(8,128)(2,1)} fusion(bf16[8192,4096]{1,0:T(8,128)(2,1)} %bitcast.3, bf16[8192,128]{1,0:T(8,128)(2,1)} %all-gather.4.cloned.1.call-done), kind=kOutput, calls=%fused_computation.10 | convolution fusion | flops 8590458880 | bytes 70254592 | tf_op jit(solution)/shard_map/dot_general | solution.py:105
  229.7 28.3 %reduce-scatter.4.cloned.1.call-done = bf16[1024,128]{1,0:T(8,128)(2,1)} async-done(((bf16[4096,128]{1,0:T(8,128)(2,1)}), bf16[1024,128]{1,0:T(8,128)(2,1)}) %reduce-scatter.4.cloned.1.call-update) | async-done | bytes 262160 | tf_op jit(solution)/shard_map/reduce_scatter | solution.py:104
  259.2 38.9 %all-reduce.2 = (f32[128]{0:T(128)S(1)}, f32[128]{0:T(128)S(1)}) all-reduce(f32[128]{0:T(128)S(1)} %get-tuple-element.63, f32[128]{0:T(128)S(1)} %get-tuple-element.62), channel_id=1, replica_groups=mesh['row'=4,'col'=8] {'row','col'}, use_global_device_ids=true, to_apply=%region_6.7 | all-reduce | flops 256 | bytes 2048 | tf_op jit(solution)/shard_map/psum | solution.py:114
  300.0 27.6 %all-gather.6.cloned.1.call-done = bf16[8192,128]{1,0:T(8,128)(2,1)} async-done(((bf16[1024,128]{1,0:T(8,128)(2,1)}), bf16[8192,128]{1,0:T(8,128)(2,1)}) %all-gather.6.cloned.1.call-update) | async-done | bytes 2097168 | tf_op jit(solution)/shard_map/all_gather | solution.py:102
  327.6 29.1 %convolution_convert_fusion.1 = bf16[4096,128]{1,0:T(8,128)(2,1)} fusion(bf16[8192,4096]{1,0:T(8,128)(2,1)} %bitcast.3, bf16[8192,128]{1,0:T(8,128)(2,1)} %all-gather.6.cloned.1.call-done), kind=kOutput, calls=%fused_computation.9 | convolution fusion | flops 8590458880 | bytes 70254592 | tf_op jit(solution)/shard_map/dot_general | solution.py:105
  356.8 27.4 %reduce-scatter.6.cloned.1.call-done = bf16[1024,128]{1,0:T(8,128)(2,1)} async-done(((bf16[4096,128]{1,0:T(8,128)(2,1)}), bf16[1024,128]{1,0:T(8,128)(2,1)}) %reduce-scatter.6.cloned.1.call-update) | async-done | bytes 262160 | tf_op jit(solution)/shard_map/reduce_scatter | solution.py:104
  385.3 38.7 %all-reduce.1 = (f32[128]{0:T(128)S(1)}, f32[128]{0:T(128)S(1)}) all-reduce(f32[128]{0:T(128)S(1)} %get-tuple-element.61, f32[128]{0:T(128)S(1)} %get-tuple-element.60), channel_id=1, replica_groups=mesh['row'=4,'col'=8] {'row','col'}, use_global_device_ids=true, to_apply=%region_13.14 | all-reduce | flops 256 | bytes 2048 | tf_op jit(solution)/shard_map/psum | solution.py:114
  424.1 1.9 fusion.9
  426.3 27.4 %all-gather.8.cloned.1.call-done = bf16[8192,128]{1,0:T(8,128)(2,1)} async-done(((bf16[1024,128]{1,0:T(8,128)(2,1)}), bf16[8192,128]{1,0:T(8,128)(2,1)}) %all-gather.8.cloned.1.call-update) | async-done | bytes 2097168 | tf_op jit(solution)/shard_map/all_gather | solution.py:102
  453.7 29.1 %convolution_convert_fusion = bf16[4096,128]{1,0:T(8,128)(2,1)} fusion(bf16[8192,4096]{1,0:T(8,128)(2,1)} %bitcast.3, bf16[8192,128]{1,0:T(8,128)(2,1)} %all-gather.8.cloned.1.call-done), kind=kOutput, calls=%fused_computation.8 | convolution fusion | flops 8590458880 | bytes 70254592 | tf_op jit(solution)/shard_map/dot_general | solution.py:105
  482.8 27.4 %reduce-scatter.8.cloned.1.call-done = bf16[1024,128]{1,0:T(8,128)(2,1)} async-done(((bf16[4096,128]{1,0:T(8,128)(2,1)}), bf16[1024,128]{1,0:T(8,128)(2,1)}) %reduce-scatter.8.cloned.1.call-update) | async-done | bytes 262160 | tf_op jit(solution)/shard_map/reduce_scatter | solution.py:104
  511.4 38.7 %all-reduce = (f32[128]{0:T(128)S(1)}, f32[128]{0:T(128)S(1)}) all-reduce(f32[128]{0:T(128)S(1)} %get-tuple-element.59, f32[128]{0:T(128)S(1)} %get-tuple-element.58), channel_id=1, replica_groups=mesh['row'=4,'col'=8] {'row','col'}, use_global_device_ids=true, to_apply=%region_18.19 | all-reduce | flops 256 | bytes 2048 | tf_op jit(solution)/shard_map/psum | solution.py:114
  550.1 2.0 multiply_add_fusion.1
  (44 shorter events, 9.0 us)
Async XLA Ops:
  7.2 193.3 %all-gather.4.cloned.1.call-start = ((), (), s32[]{:S(2)}) async-start(), calls=%async_computation.3 | async-start | bytes 2359296 | tf_op jit(solution)/shard_map/all_gather | solution.py:102
  9.1 249.0 %reduce-scatter.4.cloned.1.call-start = ((), (), s32[]{:S(2)}) async-start(), calls=%async_computation.4 | async-start | bytes 1310720 | tf_op jit(solution)/shard_map/reduce_scatter | solution.py:104
  200.5 57.5 %copy-start = (s32[1024,128]{1,0:T(8,128)S(1)}, s32[1024,128]{1,0:T(8,128)}, u32[]{:S(2)}) copy-start(s32[1024,128]{1,0:T(8,128)} %param.7) | copy-start | bytes 1572868
  229.7 98.0 %all-gather.6.cloned.1.call-start = ((), (), s32[]{:S(2)}) async-start(), calls=%async_computation.5 | async-start | bytes 2359296 | tf_op jit(solution)/shard_map/all_gather | solution.py:102
  298.1 252.0 %copy-start.1 = (f32[128]{0:T(128)}, f32[128]{0:T(128)S(1)}, u32[]{:S(2)}) copy-start(f32[128]{0:T(128)S(1)} %get-tuple-element.87) | copy-start | bytes 1540
  300.0 84.3 %reduce-scatter.6.cloned.1.call-start = ((), (), s32[]{:S(2)}) async-start(), calls=%async_computation.6 | async-start | bytes 1310720 | tf_op jit(solution)/shard_map/reduce_scatter | solution.py:104
  356.8 96.9 %all-gather.8.cloned.1.call-start = ((), (), s32[]{:S(2)}) async-start(), calls=%async_computation.7 | async-start | bytes 2359296 | tf_op jit(solution)/shard_map/all_gather | solution.py:102
  426.0 84.3 %reduce-scatter.8.cloned.1.call-start = ((), (), s32[]{:S(2)}) async-start(), calls=%async_computation.8 | async-start | bytes 1310720 | tf_op jit(solution)/shard_map/reduce_scatter | solution.py:104
Sparse Core Ops, SparseCore 0:
  9.9 31.1 all-gather.3
  229.8 28.1 reduce-scatter.3
  300.1 27.5 all-gather.5
  356.9 27.2 reduce-scatter.5
  426.1 27.5 all-gather.7
  482.9 27.2 reduce-scatter.7
where the time goes:
time: 560 us; the launch traced here: 559 us
  matrix products  251 us (45%)
  blocking collectives  143 us (26%)
  waiting for transfers between devices  138 us (25%)
  between operations  14.1 us (3%)
  other arithmetic  12.3 us (2%)
    dot_general x16, matrix products, kernel_block(): lax.dot_general(left_points, right_points, (((0,), (0,)), ((), ())), prec...  163 us
    psum x3, blocking collectives, per_device(): curvature = lax.psum(jnp.sum(direction * image, axis=0), ('row', 'col'))  116 us
    dot_general x3, matrix products, per_device(): lax.dot_general(cached, gathered, (((0,), (0,)), ((), ())), preferred_ele...  87.4 us
    reduce_scatter x3, waiting for transfers between devices, per_device(): lax.psum_scatter(lax.dot_general(cached, gathered, (((0,), (0,)), ((), ()...  83.2 us
    all_gather x3, waiting for transfers between devices, per_device(): gathered = lax.all_gather(vector_half, 'col', axis=0, tiled=True)  55.1 us
    all_gather x1, blocking collectives, per_device(): col_points = lax.all_gather(scaled, 'row', axis=1, tiled=True)  15.6 us
  transfers between devices with their start and end apart: 6, of which 5 were waited for; matrix products, arithmetic and copies ran while one was open for 29% of the time, Pallas kernels for 0%

commit v1 on v0

--- a/solution.py
+++ b/solution.py
@@ -111,7 +111,9 @@
             ).astype(jnp.float32)
             + noise_level * direction
         )
-        curvature = lax.psum(jnp.sum(direction * image, axis=0), ("row", "col"))
+        curvature = jnp.sum(
+            lax.all_gather(jnp.sum(direction * image, axis=0), ("row", "col")), axis=0
+        )
         beta_now = jnp.sqrt(squares + epsilon)
         alpha_now = curvature / (beta_now * beta_now)
         alpha_list.append(alpha_now)

time: 560 us -> 673 us (1.20)
  blocking collectives: 143 us -> 254 us
    all_gather x0 -> x3, blocking collectives: none -> 117 us  [per_device(): lax.all_gather(jnp.sum(direction * image, axis=0), ('row', 'col'))]
  transfers between devices with their start and end apart: 6 -> 6, of which waited for: 5 -> 5; matrix products, arithmetic and copies ran while one was open for 29% -> 25% of each run, Pallas kernels for 0% -> 0%
where the time goes in v1:
time: 673 us; the launch traced here: 672 us
  blocking collectives  254 us (38%)
  matrix products  251 us (37%)
  waiting for transfers between devices  140 us (21%)
  between operations  14.1 us (2%)
  other arithmetic  12.5 us (2%)
    dot_general x16, matrix products, kernel_block(): lax.dot_general(left_points, right_points, (((0,), (0,)), ((), ())), prec...  163 us
    all_gather x3, blocking collectives, per_device(): lax.all_gather(jnp.sum(direction * image, axis=0), ('row', 'col'))  117 us
    psum x3, blocking collectives, per_device(): squares = lax.psum(jnp.sum(direction * direction, axis=0), ('row', 'col'))  110 us
    dot_general x3, matrix products, per_device(): lax.dot_general(cached, gathered, (((0,), (0,)), ((), ())), preferred_ele...  87.4 us
    reduce_scatter x3, waiting for transfers between devices, per_device(): lax.psum_scatter(lax.dot_general(cached, gathered, (((0,), (0,)), ((), ()...  83.2 us
    all_gather x3, waiting for transfers between devices, per_device(): gathered = lax.all_gather(vector_half, 'col', axis=0, tiled=True)  56.4 us
    all_gather x1, blocking collectives, per_device(): col_points = lax.all_gather(scaled, 'row', axis=1, tiled=True)  15.6 us
  transfers between devices with their start and end apart: 6, of which 5 were waited for; matrix products, arithmetic and copies ran while one was open for 25% of the time, Pallas kernels for 0%

profile of v1, /device:TPU:0, one launch (start us, length us, event | category | flops | bytes accessed | tf_op | source)
XLA Modules:
  0.0 671.9 jit_solution(11850528129935099341)
XLA Ops:
  10.0 15.6 %all_gather.34 = f32[16,4096]{1,0:T(8,128)S(1)} all-gather(f32[16,1024]{1,0:T(8,128)S(1)} %broadcast_multiply_fusion), channel_id=1, replica_groups=mesh['row'=4,'col'=8] {'row'}, dimensions={1}, use_global_device_ids=true | all-gather | bytes 327680 | tf_op jit(solution)/shard_map/all_gather | solution.py:93
  25.7 11.0 %all_gather.33 = f32[16,8192]{1,0:T(8,128)S(1)} all-gather(f32[16,1024]{1,0:T(8,128)S(1)} %broadcast_multiply_fusion), channel_id=1, replica_groups=mesh['row'=4,'col'=8] {'col'}, dimensions={1}, use_global_device_ids=true | all-gather | bytes 589824 | tf_op jit(solution)/shard_map/all_gather | solution.py:92
  36.8 163.7 %while.12 = (s32[]{:T(128)}, bf16[16,512,4096]{2,1,0:T(8,128)(2,1)}, f32[16,16,512]{2,1,0:T(8,128)S(1)}, f32[4096]{0:T(1024)S(1)}, f32[16,4096]{1,0:T(8,128)S(1)}, /*index=5*/s32[]{:T(128)}) while((s32[]{:T(128)}, bf16[16,512,4096]{2,1,0:T(8,128)(2,1)}, f32[16,16,512]{2,1,0:T(8,128)S(1)}, f32[4096]{0:T(1024)S(1)}, f32[16,4096]{1,0:T(8,128)S(1)}, ...), condition=%wide.region_3.4_spmd, body=%wide.region_1.3_spmd.sunk | while | flops 415251968 | bytes 4543561 | solution.py:33
  36.8 10.2 %fusion.25 = bf16[16,512,4096]{2,1,0:T(8,128)(2,1)} fusion(bf16[16,512,4096]{2,1,0:T(8,128)(2,1)} %get-tuple-element.121, s32[]{:T(128)} %get-tuple-element.120, f32[16,4096]{1,0:T(8,128)S(1)} %get-tuple-element.130, f32[4096]{0:T(1024)S(1)} %get-tuple-element.129, f32[512]{0:T(512)S(1)} %fusion.24, f32[16,16,512]{2,1,0:T(8,128)S(1)} %get-tuple-element.128), kind=kOutput, calls=%fused_computation.2.clone.1 | convolution fusion | flops 415236096 | bytes 4508672 | tf_op jit(solution)/shard_map/while/body/eval_jaxpr/dot_general | solution.py:14
  47.1 10.2 %fusion.25 = bf16[16,512,4096]{2,1,0:T(8,128)(2,1)} fusion(bf16[16,512,4096]{2,1,0:T(8,128)(2,1)} %get-tuple-element.121, s32[]{:T(128)} %get-tuple-element.120, f32[16,4096]{1,0:T(8,128)S(1)} %get-tuple-element.130, f32[4096]{0:T(1024)S(1)} %get-tuple-element.129, f32[512]{0:T(512)S(1)} %fusion.24, f32[16,16,512]{2,1,0:T(8,128)S(1)} %get-tuple-element.128), kind=kOutput, calls=%fused_computation.2.clone.1 | convolution fusion | flops 415236096 | bytes 4508672 | tf_op jit(solution)/shard_map/while/body/eval_jaxpr/dot_general | solution.py:14
  57.3 10.2 %fusion.25 = bf16[16,512,4096]{2,1,0:T(8,128)(2,1)} fusion(bf16[16,512,4096]{2,1,0:T(8,128)(2,1)} %get-tuple-element.121, s32[]{:T(128)} %get-tuple-element.120, f32[16,4096]{1,0:T(8,128)S(1)} %get-tuple-element.130, f32[4096]{0:T(1024)S(1)} %get-tuple-element.129, f32[512]{0:T(512)S(1)} %fusion.24, f32[16,16,512]{2,1,0:T(8,128)S(1)} %get-tuple-element.128), kind=kOutput, calls=%fused_computation.2.clone.1 | convolution fusion | flops 415236096 | bytes 4508672 | tf_op jit(solution)/shard_map/while/body/eval_jaxpr/dot_general | solution.py:14
  67.5 10.2 %fusion.25 = bf16[16,512,4096]{2,1,0:T(8,128)(2,1)} fusion(bf16[16,512,4096]{2,1,0:T(8,128)(2,1)} %get-tuple-element.121, s32[]{:T(128)} %get-tuple-element.120, f32[16,4096]{1,0:T(8,128)S(1)} %get-tuple-element.130, f32[4096]{0:T(1024)S(1)} %get-tuple-element.129, f32[512]{0:T(512)S(1)} %fusion.24, f32[16,16,512]{2,1,0:T(8,128)S(1)} %get-tuple-element.128), kind=kOutput, calls=%fused_computation.2.clone.1 | convolution fusion | flops 415236096 | bytes 4508672 | tf_op jit(solution)/shard_map/while/body/eval_jaxpr/dot_general | solution.py:14
  77.8 10.2 %fusion.25 = bf16[16,512,4096]{2,1,0:T(8,128)(2,1)} fusion(bf16[16,512,4096]{2,1,0:T(8,128)(2,1)} %get-tuple-element.121, s32[]{:T(128)} %get-tuple-element.120, f32[16,4096]{1,0:T(8,128)S(1)} %get-tuple-element.130, f32[4096]{0:T(1024)S(1)} %get-tuple-element.129, f32[512]{0:T(512)S(1)} %fusion.24, f32[16,16,512]{2,1,0:T(8,128)S(1)} %get-tuple-element.128), kind=kOutput, calls=%fused_computation.2.clone.1 | convolution fusion | flops 415236096 | bytes 4508672 | tf_op jit(solution)/shard_map/while/body/eval_jaxpr/dot_general | solution.py:14
  88.0 10.2 %fusion.25 = bf16[16,512,4096]{2,1,0:T(8,128)(2,1)} fusion(bf16[16,512,4096]{2,1,0:T(8,128)(2,1)} %get-tuple-element.121, s32[]{:T(128)} %get-tuple-element.120, f32[16,4096]{1,0:T(8,128)S(1)} %get-tuple-element.130, f32[4096]{0:T(1024)S(1)} %get-tuple-element.129, f32[512]{0:T(512)S(1)} %fusion.24, f32[16,16,512]{2,1,0:T(8,128)S(1)} %get-tuple-element.128), kind=kOutput, calls=%fused_computation.2.clone.1 | convolution fusion | flops 415236096 | bytes 4508672 | tf_op jit(solution)/shard_map/while/body/eval_jaxpr/dot_general | solution.py:14
  98.2 10.2 %fusion.25 = bf16[16,512,4096]{2,1,0:T(8,128)(2,1)} fusion(bf16[16,512,4096]{2,1,0:T(8,128)(2,1)} %get-tuple-element.121, s32[]{:T(128)} %get-tuple-element.120, f32[16,4096]{1,0:T(8,128)S(1)} %get-tuple-element.130, f32[4096]{0:T(1024)S(1)} %get-tuple-element.129, f32[512]{0:T(512)S(1)} %fusion.24, f32[16,16,512]{2,1,0:T(8,128)S(1)} %get-tuple-element.128), kind=kOutput, calls=%fused_computation.2.clone.1 | convolution fusion | flops 415236096 | bytes 4508672 | tf_op jit(solution)/shard_map/while/body/eval_jaxpr/dot_general | solution.py:14
  108.4 10.2 %fusion.25 = bf16[16,512,4096]{2,1,0:T(8,128)(2,1)} fusion(bf16[16,512,4096]{2,1,0:T(8,128)(2,1)} %get-tuple-element.121, s32[]{:T(128)} %get-tuple-element.120, f32[16,4096]{1,0:T(8,128)S(1)} %get-tuple-element.130, f32[4096]{0:T(1024)S(1)} %get-tuple-element.129, f32[512]{0:T(512)S(1)} %fusion.24, f32[16,16,512]{2,1,0:T(8,128)S(1)} %get-tuple-element.128), kind=kOutput, calls=%fused_computation.2.clone.1 | convolution fusion | flops 415236096 | bytes 4508672 | tf_op jit(solution)/shard_map/while/body/eval_jaxpr/dot_general | solution.py:14
  118.6 10.3 %fusion.25 = bf16[16,512,4096]{2,1,0:T(8,128)(2,1)} fusion(bf16[16,512,4096]{2,1,0:T(8,128)(2,1)} %get-tuple-element.121, s32[]{:T(128)} %get-tuple-element.120, f32[16,4096]{1,0:T(8,128)S(1)} %get-tuple-element.130, f32[4096]{0:T(1024)S(1)} %get-tuple-element.129, f32[512]{0:T(512)S(1)} %fusion.24, f32[16,16,512]{2,1,0:T(8,128)S(1)} %get-tuple-element.128), kind=kOutput, calls=%fused_computation.2.clone.1 | convolution fusion | flops 415236096 | bytes 4508672 | tf_op jit(solution)/shard_map/while/body/eval_jaxpr/dot_general | solution.py:14
  128.9 10.2 %fusion.25 = bf16[16,512,4096]{2,1,0:T(8,128)(2,1)} fusion(bf16[16,512,4096]{2,1,0:T(8,128)(2,1)} %get-tuple-element.121, s32[]{:T(128)} %get-tuple-element.120, f32[16,4096]{1,0:T(8,128)S(1)} %get-tuple-element.130, f32[4096]{0:T(1024)S(1)} %get-tuple-element.129, f32[512]{0:T(512)S(1)} %fusion.24, f32[16,16,512]{2,1,0:T(8,128)S(1)} %get-tuple-element.128), kind=kOutput, calls=%fused_computation.2.clone.1 | convolution fusion | flops 415236096 | bytes 4508672 | tf_op jit(solution)/shard_map/while/body/eval_jaxpr/dot_general | solution.py:14
  149.4 10.2 %fusion.25 = bf16[16,512,4096]{2,1,0:T(8,128)(2,1)} fusion(bf16[16,512,4096]{2,1,0:T(8,128)(2,1)} %get-tuple-element.121, s32[]{:T(128)} %get-tuple-element.120, f32[16,4096]{1,0:T(8,128)S(1)} %get-tuple-element.130, f32[4096]{0:T(1024)S(1)} %get-tuple-element.129, f32[512]{0:T(512)S(1)} %fusion.24, f32[16,16,512]{2,1,0:T(8,128)S(1)} %get-tuple-element.128), kind=kOutput, calls=%fused_computation.2.clone.1 | convolution fusion | flops 415236096 | bytes 4508672 | tf_op jit(solution)/shard_map/while/body/eval_jaxpr/dot_general | solution.py:14
  159.6 10.3 %fusion.25 = bf16[16,512,4096]{2,1,0:T(8,128)(2,1)} fusion(bf16[16,512,4096]{2,1,0:T(8,128)(2,1)} %get-tuple-element.121, s32[]{:T(128)} %get-tuple-element.120, f32[16,4096]{1,0:T(8,128)S(1)} %get-tuple-element.130, f32[4096]{0:T(1024)S(1)} %get-tuple-element.129, f32[512]{0:T(512)S(1)} %fusion.24, f32[16,16,512]{2,1,0:T(8,128)S(1)} %get-tuple-element.128), kind=kOutput, calls=%fused_computation.2.clone.1 | convolution fusion | flops 415236096 | bytes 4508672 | tf_op jit(solution)/shard_map/while/body/eval_jaxpr/dot_general | solution.py:14
  169.9 10.2 %fusion.25 = bf16[16,512,4096]{2,1,0:T(8,128)(2,1)} fusion(bf16[16,512,4096]{2,1,0:T(8,128)(2,1)} %get-tuple-element.121, s32[]{:T(128)} %get-tuple-element.120, f32[16,4096]{1,0:T(8,128)S(1)} %get-tuple-element.130, f32[4096]{0:T(1024)S(1)} %get-tuple-element.129, f32[512]{0:T(512)S(1)} %fusion.24, f32[16,16,512]{2,1,0:T(8,128)S(1)} %get-tuple-element.128), kind=kOutput, calls=%fused_computation.2.clone.1 | convolution fusion | flops 415236096 | bytes 4508672 | tf_op jit(solution)/shard_map/while/body/eval_jaxpr/dot_general | solution.py:14
  180.1 10.2 %fusion.25 = bf16[16,512,4096]{2,1,0:T(8,128)(2,1)} fusion(bf16[16,512,4096]{2,1,0:T(8,128)(2,1)} %get-tuple-element.121, s32[]{:T(128)} %get-tuple-element.120, f32[16,4096]{1,0:T(8,128)S(1)} %get-tuple-element.130, f32[4096]{0:T(1024)S(1)} %get-tuple-element.129, f32[512]{0:T(512)S(1)} %fusion.24, f32[16,16,512]{2,1,0:T(8,128)S(1)} %get-tuple-element.128), kind=kOutput, calls=%fused_computation.2.clone.1 | convolution fusion | flops 415236096 | bytes 4508672 | tf_op jit(solution)/shard_map/while/body/eval_jaxpr/dot_general | solution.py:14
  190.3 10.2 %fusion.25 = bf16[16,512,4096]{2,1,0:T(8,128)(2,1)} fusion(bf16[16,512,4096]{2,1,0:T(8,128)(2,1)} %get-tuple-element.121, s32[]{:T(128)} %get-tuple-element.120, f32[16,4096]{1,0:T(8,128)S(1)} %get-tuple-element.130, f32[4096]{0:T(1024)S(1)} %get-tuple-element.129, f32[512]{0:T(512)S(1)} %fusion.24, f32[16,16,512]{2,1,0:T(8,128)S(1)} %get-tuple-element.128), kind=kOutput, calls=%fused_computation.2.clone.1 | convolution fusion | flops 415236096 | bytes 4508672 | tf_op jit(solution)/shard_map/while/body/eval_jaxpr/dot_general | solution.py:14
  200.5 29.2 %convolution_convert_fusion.2 = bf16[4096,128]{1,0:T(8,128)(2,1)} fusion(bf16[8192,4096]{1,0:T(8,128)(2,1)} %bitcast.3, bf16[8192,128]{1,0:T(8,128)(2,1)} %all-gather.10.cloned.1.call-done), kind=kOutput, calls=%fused_computation.10 | convolution fusion | flops 8590458880 | bytes 70254592 | tf_op jit(solution)/shard_map/dot_general | solution.py:105
  229.7 28.3 %reduce-scatter.4.cloned.1.call-done = bf16[1024,128]{1,0:T(8,128)(2,1)} async-done(((bf16[4096,128]{1,0:T(8,128)(2,1)}), bf16[1024,128]{1,0:T(8,128)(2,1)}) %reduce-scatter.4.cloned.1.call-update) | async-done | bytes 262160 | tf_op jit(solution)/shard_map/reduce_scatter | solution.py:104
  259.2 39.2 %all-gather.3 = f32[32,1,128]{2,1,0:T(1,128)S(1)} all-gather(f32[1,1,128]{2,1,0:T(1,128)S(1)} %bitcast.39), channel_id=2, replica_groups=mesh['row'=4,'col'=8] {'row','col'}, dimensions={0}, use_global_device_ids=true | all-gather | bytes 16896 | tf_op jit(solution)/shard_map/all_gather | solution.py:115
  298.4 36.8 %psum.21 = f32[128]{0:T(128)S(1)} all-reduce(f32[128]{0:T(128)S(1)} %get-tuple-element.62), channel_id=1, replica_groups=mesh['row'=4,'col'=8] {'row','col'}, use_global_device_ids=true, to_apply=%region_8.9 | all-reduce | flops 128 | bytes 1024 | tf_op jit(solution)/shard_map/psum | solution.py:100
  337.2 28.3 %all-gather.12.cloned.1.call-done = bf16[8192,128]{1,0:T(8,128)(2,1)} async-done(((bf16[1024,128]{1,0:T(8,128)(2,1)}), bf16[8192,128]{1,0:T(8,128)(2,1)}) %all-gather.12.cloned.1.call-update) | async-done | bytes 2097168 | tf_op jit(solution)/shard_map/all_gather | solution.py:102
  365.5 29.1 %convolution_convert_fusion.1 = bf16[4096,128]{1,0:T(8,128)(2,1)} fusion(bf16[8192,4096]{1,0:T(8,128)(2,1)} %bitcast.3, bf16[8192,128]{1,0:T(8,128)(2,1)} %all-gather.12.cloned.1.call-done), kind=kOutput, calls=%fused_computation.9 | convolution fusion | flops 8590458880 | bytes 70254592 | tf_op jit(solution)/shard_map/dot_general | solution.py:105
  394.7 27.4 %reduce-scatter.6.cloned.1.call-done = bf16[1024,128]{1,0:T(8,128)(2,1)} async-done(((bf16[4096,128]{1,0:T(8,128)(2,1)}), bf16[1024,128]{1,0:T(8,128)(2,1)}) %reduce-scatter.6.cloned.1.call-update) | async-done | bytes 262160 | tf_op jit(solution)/shard_map/reduce_scatter | solution.py:104
  423.2 39.0 %all-gather.4 = f32[32,1,128]{2,1,0:T(1,128)S(1)} all-gather(f32[1,1,128]{2,1,0:T(1,128)S(1)} %bitcast.40), channel_id=3, replica_groups=mesh['row'=4,'col'=8] {'row','col'}, dimensions={0}, use_global_device_ids=true | all-gather | bytes 16896 | tf_op jit(solution)/shard_map/all_gather | solution.py:115
  462.3 36.8 %psum.22 = f32[128]{0:T(128)S(1)} all-reduce(f32[128]{0:T(128)S(1)} %get-tuple-element.60), channel_id=1, replica_groups=mesh['row'=4,'col'=8] {'row','col'}, use_global_device_ids=true, to_apply=%region_10.11 | all-reduce | flops 128 | bytes 1024 | tf_op jit(solution)/shard_map/psum | solution.py:100
  501.3 28.1 %all-gather.14.cloned.1.call-done = bf16[8192,128]{1,0:T(8,128)(2,1)} async-done(((bf16[1024,128]{1,0:T(8,128)(2,1)}), bf16[8192,128]{1,0:T(8,128)(2,1)}) %all-gather.14.cloned.1.call-update) | async-done | bytes 2097168 | tf_op jit(solution)/shard_map/all_gather | solution.py:102
  529.4 29.1 %convolution_convert_fusion = bf16[4096,128]{1,0:T(8,128)(2,1)} fusion(bf16[8192,4096]{1,0:T(8,128)(2,1)} %bitcast.3, bf16[8192,128]{1,0:T(8,128)(2,1)} %all-gather.14.cloned.1.call-done), kind=kOutput, calls=%fused_computation.8 | convolution fusion | flops 8590458880 | bytes 70254592 | tf_op jit(solution)/shard_map/dot_general | solution.py:105
  558.5 27.4 %reduce-scatter.8.cloned.1.call-done = bf16[1024,128]{1,0:T(8,128)(2,1)} async-done(((bf16[4096,128]{1,0:T(8,128)(2,1)}), bf16[1024,128]{1,0:T(8,128)(2,1)}) %reduce-scatter.8.cloned.1.call-update) | async-done | bytes 262160 | tf_op jit(solution)/shard_map/reduce_scatter | solution.py:104
  587.1 39.0 %all-gather.5 = f32[32,1,128]{2,1,0:T(1,128)S(1)} all-gather(f32[1,1,128]{2,1,0:T(1,128)S(1)} %bitcast.38), channel_id=4, replica_groups=mesh['row'=4,'col'=8] {'row','col'}, dimensions={0}, use_global_device_ids=true | all-gather | bytes 16896 | tf_op jit(solution)/shard_map/all_gather | solution.py:115
  626.2 36.8 %psum.23 = f32[128]{0:T(128)S(1)} all-reduce(f32[128]{0:T(128)S(1)} %get-tuple-element.58), channel_id=1, replica_groups=mesh['row'=4,'col'=8] {'row','col'}, use_global_device_ids=true, to_apply=%region_15.16 | all-reduce | flops 128 | bytes 1024 | tf_op jit(solution)/shard_map/psum | solution.py:100
  (50 shorter events, 23.3 us)
Async XLA Ops:
  7.2 193.3 %all-gather.10.cloned.1.call-start = ((), (), s32[]{:S(2)}) async-start(), calls=%async_computation.3 | async-start | bytes 2359296 | tf_op jit(solution)/shard_map/all_gather | solution.py:102
  9.1 249.0 %reduce-scatter.4.cloned.1.call-start = ((), (), s32[]{:S(2)}) async-start(), calls=%async_computation.4 | async-start | bytes 1310720 | tf_op jit(solution)/shard_map/reduce_scatter | solution.py:104
  200.5 57.5 %copy-start = (s32[1024,128]{1,0:T(8,128)S(1)}, s32[1024,128]{1,0:T(8,128)}, u32[]{:S(2)}) copy-start(s32[1024,128]{1,0:T(8,128)} %param.7) | copy-start | bytes 1572868
  229.7 135.8 %all-gather.12.cloned.1.call-start = ((), (), s32[]{:S(2)}) async-start(), calls=%async_computation.5 | async-start | bytes 2359296 | tf_op jit(solution)/shard_map/all_gather | solution.py:102
  335.2 327.8 %copy-start.1 = (f32[128]{0:T(128)}, f32[128]{0:T(128)S(1)}, u32[]{:S(2)}) copy-start(f32[128]{0:T(128)S(1)} %get-tuple-element.81) | copy-start | bytes 1540
  337.1 84.9 %reduce-scatter.6.cloned.1.call-start = ((), (), s32[]{:S(2)}) async-start(), calls=%async_computation.6 | async-start | bytes 1310720 | tf_op jit(solution)/shard_map/reduce_scatter | solution.py:104
  394.6 134.8 %all-gather.14.cloned.1.call-start = ((), (), s32[]{:S(2)}) async-start(), calls=%async_computation.7 | async-start | bytes 2359296 | tf_op jit(solution)/shard_map/all_gather | solution.py:102
  501.0 84.9 %reduce-scatter.8.cloned.1.call-start = ((), (), s32[]{:S(2)}) async-start(), calls=%async_computation.8 | async-start | bytes 1310720 | tf_op jit(solution)/shard_map/reduce_scatter | solution.py:104
Sparse Core Ops, SparseCore 0:
  9.9 31.1 all-gather.9
  229.8 28.1 reduce-scatter.3
  337.2 28.1 all-gather.11
  394.7 27.2 reduce-scatter.5
  501.2 28.1 all-gather.13
  558.7 27.2 reduce-scatter.7
